TPU v7x, 32 devices: a whole 2x2x4 slice. The times are simulated.
32 devices in a mesh: shard: 2 (over core), cols: 4 (over y, x), job: 4 (over z).
Axes of the slice: x: 2, y: 2, z: 4, core: 2. Of those that a mesh axis runs over, the one named last changes fastest.
Arguments:
- one_query: float32 [16384, 4096], P(('job', 'shard'), 'cols'), parts along dimension 0, may hold values from -0.125 to 0.125
- other_query: float32 [16384, 4096], P(('job', 'shard'), 'cols'), parts along dimension 0, may hold values from -0.09375 to 0.09375
- one_key: float32 [16384, 1024], P(('job', 'shard'), 'cols'), parts along dimension 0, may hold values from -0.125 to 0.125
- other_key: float32 [16384, 1024], P(('job', 'shard'), 'cols'), parts along dimension 0, may hold values from -0.09375 to 0.09375
- one_value: float32 [16384, 1024], P(('job', 'shard'), 'cols'), parts along dimension 0, may hold values from -0.125 to 0.125
- other_value: float32 [16384, 1024], P(('job', 'shard'), 'cols'), parts along dimension 0, may hold values from -0.09375 to 0.09375
- mix_share: float32 [16384], P(('job', 'shard')), parts along dimension 0, may hold values from 0.2 to 0.8
- norm_gain: float32 [16384], P(('job', 'shard')), parts along dimension 0, may hold values from 0.25 to 1.75
Outputs:
- final_query: bfloat16 [16384, 4096], P('job', 'cols'), parts along dimension 0
- final_key: bfloat16 [16384, 1024], P('job', 'cols'), parts along dimension 0
- final_value: bfloat16 [16384, 1024], P('job', 'cols'), parts along dimension 0
- scale_query: float32 [16384], P(('job', 'cols')), parts along dimension 0
- scale_key: float32 [4096], P(('job', 'cols')), parts along dimension 0
- scale_value: float32 [4096], P(('job', 'cols')), parts along dimension 0
There are 4 independent parts, one for each index of `job`. A program takes and returns all parts, laid end to end along the dimension named above; each array names one. Nothing has to cross between parts.
All inputs are finite; a program needn't handle non-finite values. Where the computation divides by a largest or mean magnitude, that divisor is 1e-20 or more.
Results may differ from a plain program's by a relative error of at most 0.001.
Values may be sent and summed in bfloat16 or wider, within the bound.
No kernel may reach another device: no remote copies, remote signals or barrier semaphores. Data moves between devices by JAX's collectives and lax.ppermute only.
A program may use at most 128 MiB of HBM per device.

v0:
```python
import jax
import jax.numpy as jnp
from jax import lax
from jax.sharding import PartitionSpec as P


def shards(
    one_query, other_query, one_key, other_key, one_value, other_value, mix_share, norm_gain
):
    result_query = mix_share[:, None] * one_query + (1.0 - mix_share[:, None]) * other_query
    result_key = mix_share[:, None] * one_key + (1.0 - mix_share[:, None]) * other_key
    result_value = mix_share[:, None] * one_value + (1.0 - mix_share[:, None]) * other_value
    result_gained_query = result_query * norm_gain[:, None]
    result_gained_key = result_key * norm_gain[:, None]
    result_gained_value = result_value * norm_gain[:, None]
    scale_query, scale_key, scale_value = lax.pmax(
        (
            jnp.max(jnp.abs(result_gained_query), axis=0),
            jnp.max(jnp.abs(result_gained_key), axis=0),
            jnp.max(jnp.abs(result_gained_value), axis=0),
        ),
        "shard",
    )
    narrow_query, narrow_key, narrow_value = (
        (result_gained_query / scale_query).astype(jnp.bfloat16),
        (result_gained_key / scale_key).astype(jnp.bfloat16),
        (result_gained_value / scale_value).astype(jnp.bfloat16),
    )
    final_query, final_key, final_value = (
        lax.all_gather(narrow_query, "shard", axis=0, tiled=True),
        lax.all_gather(narrow_key, "shard", axis=0, tiled=True),
        lax.all_gather(narrow_value, "shard", axis=0, tiled=True),
    )
    return (final_query, final_key, final_value, scale_query, scale_key, scale_value)


def solution(mesh):
    placed = (
        P(("job", "shard"), "cols"),
        P(("job", "shard"), "cols"),
        P(("job", "shard"), "cols"),
        P(("job", "shard"), "cols"),
        P(("job", "shard"), "cols"),
        P(("job", "shard"), "cols"),
        P(("job", "shard")),
        P(("job", "shard")),
    )
    return jax.shard_map(
        shards,
        mesh=mesh,
        in_specs=placed,
        out_specs=(
            P("job", "cols"),
            P("job", "cols"),
            P("job", "cols"),
            P(("job", "cols")),
            P(("job", "cols")),
            P(("job", "cols")),
        ),
        check_vma=False,
    )
```

profile of v0, /device:TPU:0, one launch (start us, length us, event | category | flops | bytes accessed | tf_op | source)
XLA Modules:
  0.0 94.1 jit_solution(1859230134611936218)
XLA Ops:
  7.2 0.0 all-gather.6.cloned.1.call-start
  7.2 0.7 broadcast_subtract_fusion
  7.9 0.0 copy-start.2
  7.9 0.0 copy-start.3
  7.9 0.0 copy-start.4
  7.9 0.0 copy-start.5
  7.9 0.0 copy-start.6
  7.9 0.0 copy-start.7
  8.0 10.3 %abs_reduce_fusion = (f32[1024]{0:T(1024)S(1)}, f32[2048,1024]{1,0:T(8,128)}) fusion(f32[2048]{0:T(1024)} %param.15, f32[2048,1024]{1,0:T(8,128)} %param.9, f32[2048]{0:T(1024)S(1)} %broadcast_subtract_fusion, f32[2048,1024]{1,0:T(8,128)} %param.8, f32[2048]{0:T(1024)} %param.14), kind=kLoop, calls=%fused_computation.1 | loop fusion | flops 12581888 | bytes 25194496 | tf_op jit(solution)/shard_map/reduce_max | solution.py:18
  18.3 0.0 copy-done.2
  18.3 0.0 copy-done.3
  18.3 0.0 copy-done.4
  18.3 0.7 copy-done.5
  19.0 0.0 copy-done.6
  19.0 0.0 copy-done.7
  19.0 1.9 %abs_reduce_fusion.1 = (f32[256]{0:T(256)S(1)}, f32[2048,256]{1,0:T(8,128)S(1)}, f32[256]{0:T(256)S(1)}, f32[2048,256]{1,0:T(8,128)}) fusion(f32[2048]{0:T(1024)S(1)} %copy-done.7, f32[2048,256]{1,0:T(8,128)S(1)} %copy-done.2, f32[2048]{0:T(1024)S(1)} %broadcast_subtract_fusion, f32[2048,256]{1,0:T(8,128)S(1)} %copy-done.3, f32[2048]{0:T(1024)S(1)} %copy-done.6, ...), kind=kLoop, calls=%fused_computation.4 | loop fusion | flops 6290944 | bytes 12609536 | tf_op jit(solution)/shard_map/reduce_max | solution.py:20
  21.0 2.6 %all-reduce = (f32[1024]{0:T(1024)S(1)}, f32[256]{0:T(256)S(1)}, f32[256]{0:T(256)S(1)}) all-reduce(f32[1024]{0:T(1024)S(1)} %get-tuple-element.13, f32[256]{0:T(256)S(1)} %get-tuple-element.15, f32[256]{0:T(256)S(1)} %get-tuple-element.9), channel_id=1, replica_groups=mesh['shard'=2,'cols'=4,'job'=4] {'shard'}, use_global_device_ids=true, to_apply=%region_1.0 | all-reduce | flops 1536 | bytes 12288 | tf_op jit(solution)/shard_map/pmax | solution.py:16
  23.6 0.0 copy-start.9
  23.6 0.0 copy-start.10
  23.6 0.0 copy-start.8
  23.6 2.7 %divide_convert_fusion.2 = bf16[2048,256]{1,0:T(8,128)(2,1)} fusion(f32[2048,256]{1,0:T(8,128)} %get-tuple-element.16, f32[256]{0:T(256)S(1)} %get-tuple-element.27), kind=kLoop, calls=%fused_computation.6 | loop fusion | flops 1048576 | bytes 3146752 | tf_op jit(solution)/shard_map/convert_element_type | solution.py:26
  26.3 0.0 all-gather.6.cloned.1.call-update
  26.4 0.0 copy-done.9
  26.4 0.0 all-gather.8.cloned.1.call-start
  26.4 0.0 copy-done.10
  26.4 1.1 %divide_convert_fusion.1 = bf16[2048,256]{1,0:T(8,128)(2,1)} fusion(f32[2048,256]{1,0:T(8,128)S(1)} %get-tuple-element.10, f32[256]{0:T(256)S(1)} %get-tuple-element.28), kind=kLoop, calls=%fused_computation.3 | loop fusion | flops 1048576 | bytes 3146752 | tf_op jit(solution)/shard_map/convert_element_type | solution.py:27
  27.6 0.0 all-gather.8.cloned.1.call-update
  27.6 0.0 all-gather.4.cloned.1.call-start
  27.6 0.0 copy-done.8
  27.6 6.6 %divide_convert_fusion = bf16[2048,1024]{1,0:T(8,128)(2,1)} fusion(f32[2048,1024]{1,0:T(8,128)} %get-tuple-element.14, f32[1024]{0:T(1024)S(1)} %get-tuple-element.26), kind=kLoop, calls=%fused_computation | loop fusion | flops 4194304 | bytes 12587008 | tf_op jit(solution)/shard_map/convert_element_type | solution.py:25
  34.3 0.0 all-gather.4.cloned.1.call-update
  34.3 5.4 %all-gather.6.cloned.1.call-done = bf16[4096,256]{1,0:T(8,128)(2,1)} async-done(((bf16[2048,256]{1,0:T(8,128)(2,1)}), bf16[4096,256]{1,0:T(8,128)(2,1)}) %all-gather.6.cloned.1.call-update) | async-done | bytes 2097168 | tf_op jit(solution)/shard_map/all_gather | solution.py:31
  39.7 0.0 copy-start
  39.7 13.9 %all-gather.8.cloned.1.call-done = bf16[4096,256]{1,0:T(8,128)(2,1)} async-done(((bf16[2048,256]{1,0:T(8,128)(2,1)}), bf16[4096,256]{1,0:T(8,128)(2,1)}) %all-gather.8.cloned.1.call-update) | async-done | bytes 2097168 | tf_op jit(solution)/shard_map/all_gather | solution.py:32
  53.6 22.6 %all-gather.4.cloned.1.call-done = bf16[4096,1024]{1,0:T(8,128)(2,1)} async-done(((bf16[2048,1024]{1,0:T(8,128)(2,1)}), bf16[4096,1024]{1,0:T(8,128)(2,1)}) %all-gather.4.cloned.1.call-update) | async-done | bytes 8388624 | tf_op jit(solution)/shard_map/all_gather | solution.py:30
  76.2 7.8 %copy.17 = bf16[4096,1024]{1,0:T(8,128)(2,1)} copy(bf16[4096,1024]{1,0:T(8,128)(2,1)} %all-gather.4.cloned.1.call-done) | data formatting | bytes 16777216
  83.9 0.0 copy-done
  83.9 0.0 copy-start.1
  83.9 1.3 %copy.18 = bf16[4096,256]{1,0:T(8,128)(2,1)} copy(bf16[4096,256]{1,0:T(8,128)(2,1)S(1)} %copy-done) | data formatting | bytes 4194304
  85.2 1.0 %copy-done.1 = bf16[4096,256]{1,0:T(8,128)(2,1)S(1)} copy-done((bf16[4096,256]{1,0:T(8,128)(2,1)S(1)}, bf16[4096,256]{1,0:T(8,128)(2,1)}, u32[]{:S(2)}) %copy-start.1) | copy-done | bytes 2097176
  86.3 1.3 %copy.19 = bf16[4096,256]{1,0:T(8,128)(2,1)} copy(bf16[4096,256]{1,0:T(8,128)(2,1)S(1)} %copy-done.1) | data formatting | bytes 4194304
Async XLA Ops:
  7.2 32.5 %all-gather.6.cloned.1.call-start = ((), (), s32[]{:S(2)}) async-start(), calls=%async_computation.1 | async-start | bytes 3145728 | tf_op jit(solution)/shard_map/all_gather | solution.py:31
  7.9 10.4 %copy-start.2 = (f32[2048,256]{1,0:T(8,128)S(1)}, f32[2048,256]{1,0:T(8,128)}, u32[]{:S(2)}) copy-start(f32[2048,256]{1,0:T(8,128)} %param.13) | copy-start | bytes 6291460
  7.9 10.4 %copy-start.3 = (f32[2048,256]{1,0:T(8,128)S(1)}, f32[2048,256]{1,0:T(8,128)}, u32[]{:S(2)}) copy-start(f32[2048,256]{1,0:T(8,128)} %param.12) | copy-start | bytes 6291460
  7.9 10.4 %copy-start.4 = (f32[2048,256]{1,0:T(8,128)S(1)}, f32[2048,256]{1,0:T(8,128)}, u32[]{:S(2)}) copy-start(f32[2048,256]{1,0:T(8,128)} %param.11) | copy-start | bytes 6291460
  7.9 11.1 %copy-start.5 = (f32[2048,256]{1,0:T(8,128)S(1)}, f32[2048,256]{1,0:T(8,128)}, u32[]{:S(2)}) copy-start(f32[2048,256]{1,0:T(8,128)} %param.10) | copy-start | bytes 6291460
  7.9 11.1 %copy-start.6 = (f32[2048]{0:T(1024)S(1)}, f32[2048]{0:T(1024)}, u32[]{:S(2)}) copy-start(f32[2048]{0:T(1024)} %param.14) | copy-start | bytes 24580
  7.9 11.1 %copy-start.7 = (f32[2048]{0:T(1024)S(1)}, f32[2048]{0:T(1024)}, u32[]{:S(2)}) copy-start(f32[2048]{0:T(1024)} %param.15) | copy-start | bytes 24580
  23.6 2.8 %copy-start.9 = (f32[256]{0:T(256)}, f32[256]{0:T(256)S(1)}, u32[]{:S(2)}) copy-start(f32[256]{0:T(256)S(1)} %get-tuple-element.27) | copy-start | bytes 3076
  23.6 2.8 %copy-start.10 = (f32[256]{0:T(256)}, f32[256]{0:T(256)S(1)}, u32[]{:S(2)}) copy-start(f32[256]{0:T(256)S(1)} %get-tuple-element.28) | copy-start | bytes 3076
  23.6 4.0 %copy-start.8 = (f32[1024]{0:T(1024)}, f32[1024]{0:T(1024)S(1)}, u32[]{:S(2)}) copy-start(f32[1024]{0:T(1024)S(1)} %get-tuple-element.26) | copy-start | bytes 12292
  26.4 27.2 %all-gather.8.cloned.1.call-start = ((), (), s32[]{:S(2)}) async-start(), calls=%async_computation.2 | async-start | bytes 3145728 | tf_op jit(solution)/shard_map/all_gather | solution.py:32
  27.6 48.6 %all-gather.4.cloned.1.call-start = ((), (), s32[]{:S(2)}) async-start(), calls=%async_computation | async-start | bytes 12582912 | tf_op jit(solution)/shard_map/all_gather | solution.py:30
  39.7 44.3 %copy-start = (bf16[4096,256]{1,0:T(8,128)(2,1)S(1)}, bf16[4096,256]{1,0:T(8,128)(2,1)}, u32[]{:S(2)}) copy-start(bf16[4096,256]{1,0:T(8,128)(2,1)} %all-gather.6.cloned.1.call-done) | copy-start | bytes 6291460
  83.9 2.3 %copy-start.1 = (bf16[4096,256]{1,0:T(8,128)(2,1)S(1)}, bf16[4096,256]{1,0:T(8,128)(2,1)}, u32[]{:S(2)}) copy-start(bf16[4096,256]{1,0:T(8,128)(2,1)} %all-gather.8.cloned.1.call-done) | copy-start | bytes 6291460
Sparse Core Ops, SparseCore 0:
  26.5 13.1 all-gather.5
  41.8 11.7 all-gather.7
  55.1 21.0 all-gather.3
where the time goes:
time: 94.4 us; the launch traced here: 94.1 us
  waiting for transfers between devices  41.9 us (44%)
  other arithmetic  23.5 us (25%)
  between operations  13.8 us (15%)
  local copies, waits for them, and re-layouts  12.2 us (13%)
  blocking collectives  2.62 us (3%)
    all_gather x1, waiting for transfers between devices, shards(): lax.all_gather(narrow_query, 'shard', axis=0, tiled=True)  22.6 us
    all_gather x1, waiting for transfers between devices, shards(): lax.all_gather(narrow_value, 'shard', axis=0, tiled=True)  13.9 us
    unnamed x25, local copies, waits for them, and re-layouts  12.2 us
    reduce_max x1, other arithmetic, shards(): jnp.max(jnp.abs(result_gained_query), axis=0)  10.3 us
    convert_element_type x1, other arithmetic, shards(): (result_gained_query / scale_query).astype(jnp.bfloat16)  6.62 us
    all_gather x1, waiting for transfers between devices, shards(): lax.all_gather(narrow_key, 'shard', axis=0, tiled=True)  5.36 us
    convert_element_type x1, other arithmetic, shards(): (result_gained_key / scale_key).astype(jnp.bfloat16)  2.73 us
    pmax x1, blocking collectives, shards(): lax.pmax((jnp.max(jnp.abs(result_gained_query), axis=0), jnp.max(jnp.abs(...  2.62 us
  transfers between devices with their start and end apart: 3, of which 3 were waited for; matrix products, arithmetic and copies ran while one was open for 8% of the time, Pallas kernels for 0%

commit v1 on v0

--- a/solution.py
+++ b/solution.py
@@ -27,7 +27,10 @@
         (result_gained_value / scale_value).astype(jnp.bfloat16),
     )
     final_query, final_key, final_value = (
-        lax.all_gather(narrow_query, "shard", axis=0, tiled=True),
+        jnp.concatenate(
+            lax.all_to_all(jnp.stack([narrow_query] * lax.axis_size("shard")), "shard", 0, 0),
+            axis=0,
+        ),
         lax.all_gather(narrow_key, "shard", axis=0, tiled=True),
         lax.all_gather(narrow_value, "shard", axis=0, tiled=True),
     )

time: 94.4 us -> 75.9 us (0.80)
  waiting for transfers between devices: 41.9 us -> 0.04 us
  blocking collectives: 2.62 us -> 22.6 us
  other arithmetic: 23.5 us -> 25.6 us
    all_gather x1 -> x0, waiting for transfers between devices: 22.6 us -> none  [shards(): lax.all_gather(narrow_query, 'shard', axis=0, tiled=True)]
    all_to_all x0 -> x1, blocking collectives: none -> 20 us  [shards(): lax.all_to_all(jnp.stack([narrow_query] * lax.axis_size('shard')), 'shard...]
    all_gather x1, waiting for transfers between devices: 13.9 us -> 0.01 us  [shards(): lax.all_gather(narrow_value, 'shard', axis=0, tiled=True)]
    another operation x0 -> x2, other arithmetic: none -> 8.79 us  [shards(): jnp.stack([narrow_query] * lax.axis_size('shard'))]
    convert_element_type x1 -> x0, other arithmetic: 6.62 us -> none  [shards(): (result_gained_query / scale_query).astype(jnp.bfloat16)]
    all_gather x1, waiting for transfers between devices: 5.36 us -> 0.01 us  [shards(): lax.all_gather(narrow_key, 'shard', axis=0, tiled=True)]
  transfers between devices with their start and end apart: 3 -> 2, of which waited for: 3 -> 0; matrix products, arithmetic and copies ran while one was open for 8% -> 13% of each run, Pallas kernels for 0% -> 0%
where the time goes in v1:
time: 75.9 us; the launch traced here: 74.8 us
  other arithmetic  25.6 us (34%)
  blocking collectives  22.6 us (30%)
  between operations  14.1 us (19%)
  local copies, waits for them, and re-layouts  12.3 us (16%)
    all_to_all x1, blocking collectives, shards(): lax.all_to_all(jnp.stack([narrow_query] * lax.axis_size('shard')), 'shard...  20 us
    unnamed x25, local copies, waits for them, and re-layouts  12.3 us
    reduce_max x1, other arithmetic, shards(): jnp.max(jnp.abs(result_gained_query), axis=0)  10.3 us
    another operation x2, other arithmetic, shards(): jnp.stack([narrow_query] * lax.axis_size('shard'))  8.79 us
    convert_element_type x1, other arithmetic, shards(): (result_gained_key / scale_key).astype(jnp.bfloat16)  2.73 us
    pmax x1, blocking collectives, shards(): lax.pmax((jnp.max(jnp.abs(result_gained_query), axis=0), jnp.max(jnp.abs(...  2.62 us
    reduce_max x1, other arithmetic, shards(): jnp.max(jnp.abs(result_gained_value), axis=0)  1.95 us
  transfers between devices with their start and end apart: 2, of which 0 were waited for; matrix products, arithmetic and copies ran while one was open for 13% of the time, Pallas kernels for 0%

profile of v1, /device:TPU:0, one launch (start us, length us, event | category | flops | bytes accessed | tf_op | source)
XLA Modules:
  0.0 74.8 jit_solution(5938234592312448090)
XLA Ops:
  7.2 0.0 all-gather.3.cloned.1.call-start
  7.2 0.7 broadcast_subtract_fusion
  7.9 0.0 copy-start.2
  7.9 0.0 copy-start.3
  7.9 0.0 copy-start.4
  7.9 0.0 copy-start.5
  7.9 0.0 copy-start.6
  7.9 0.0 copy-start.7
  8.0 10.3 %abs_reduce_fusion = (f32[1024]{0:T(1024)S(1)}, f32[2048,1024]{1,0:T(8,128)}) fusion(f32[2048]{0:T(1024)} %param.15, f32[2048,1024]{1,0:T(8,128)} %param.9, f32[2048]{0:T(1024)S(1)} %broadcast_subtract_fusion, f32[2048,1024]{1,0:T(8,128)} %param.8, f32[2048]{0:T(1024)} %param.14), kind=kLoop, calls=%fused_computation.2 | loop fusion | flops 12581888 | bytes 25194496 | tf_op jit(solution)/shard_map/reduce_max | solution.py:18
  18.3 0.0 copy-done.2
  18.3 0.0 copy-done.3
  18.3 0.0 copy-done.4
  18.3 0.7 copy-done.5
  19.0 0.0 copy-done.6
  19.0 0.0 copy-done.7
  19.0 1.9 %abs_reduce_fusion.1 = (f32[256]{0:T(256)S(1)}, f32[2048,256]{1,0:T(8,128)S(1)}, f32[256]{0:T(256)S(1)}, f32[2048,256]{1,0:T(8,128)}) fusion(f32[2048]{0:T(1024)S(1)} %copy-done.7, f32[2048,256]{1,0:T(8,128)S(1)} %copy-done.2, f32[2048]{0:T(1024)S(1)} %broadcast_subtract_fusion, f32[2048,256]{1,0:T(8,128)S(1)} %copy-done.3, f32[2048]{0:T(1024)S(1)} %copy-done.6, ...), kind=kLoop, calls=%fused_computation.6 | loop fusion | flops 6290944 | bytes 12609536 | tf_op jit(solution)/shard_map/reduce_max | solution.py:20
  21.0 2.6 %all-reduce = (f32[1024]{0:T(1024)S(1)}, f32[256]{0:T(256)S(1)}, f32[256]{0:T(256)S(1)}) all-reduce(f32[1024]{0:T(1024)S(1)} %get-tuple-element.13, f32[256]{0:T(256)S(1)} %get-tuple-element.15, f32[256]{0:T(256)S(1)} %get-tuple-element.9), channel_id=1, replica_groups=mesh['shard'=2,'cols'=4,'job'=4] {'shard'}, use_global_device_ids=true, to_apply=%region_1.0 | all-reduce | flops 1536 | bytes 12288 | tf_op jit(solution)/shard_map/pmax | solution.py:16
  23.6 0.0 copy-start.9
  23.6 0.0 copy-start.10
  23.6 0.0 copy-start.8
  23.6 2.7 %divide_convert_fusion.2 = bf16[2048,256]{1,0:T(8,128)(2,1)} fusion(f32[2048,256]{1,0:T(8,128)} %get-tuple-element.16, f32[256]{0:T(256)S(1)} %get-tuple-element.27), kind=kLoop, calls=%fused_computation.8 | loop fusion | flops 1048576 | bytes 3146752 | tf_op jit(solution)/shard_map/convert_element_type | solution.py:26
  26.3 0.0 all-gather.3.cloned.1.call-update
  26.4 0.0 copy-done.9
  26.4 0.0 all-gather.5.cloned.1.call-start
  26.4 0.0 copy-done.10
  26.4 1.1 %divide_convert_fusion.1 = bf16[2048,256]{1,0:T(8,128)(2,1)} fusion(f32[2048,256]{1,0:T(8,128)S(1)} %get-tuple-element.10, f32[256]{0:T(256)S(1)} %get-tuple-element.28), kind=kLoop, calls=%fused_computation.5 | loop fusion | flops 1048576 | bytes 3146752 | tf_op jit(solution)/shard_map/convert_element_type | solution.py:27
  27.6 0.0 all-gather.5.cloned.1.call-update
  27.6 0.0 copy-done.8
  27.6 4.6 %fusion = bf16[1,2048,1024]{2,1,0:T(8,128)(2,1)S(1)} fusion(f32[2048,1024]{1,0:T(8,128)} %get-tuple-element.14, f32[1024]{0:T(1024)S(1)} %get-tuple-element.26), kind=kLoop, calls=%fused_computation.4 | loop fusion | flops 4194304 | bytes 12587008 | tf_op jit(solution)/shard_map/stack | solution.py:31
  32.3 4.1 %pad_maximum_fusion = bf16[2,2048,1024]{2,1,0:T(8,128)(2,1)} fusion(bf16[1,2048,1024]{2,1,0:T(8,128)(2,1)S(1)} %fusion), kind=kLoop, calls=%fused_computation | loop fusion | flops 4194304 | bytes 12582912 | tf_op jit(solution)/shard_map/stack | solution.py:31
  36.4 20.0 %all_to_all.5 = bf16[2,2048,1024]{2,1,0:T(8,128)(2,1)} all-to-all(bf16[2,2048,1024]{2,1,0:T(8,128)(2,1)} %pad_maximum_fusion), channel_id=1, replica_groups=mesh['shard'=2,'cols'=4,'job'=4] {'shard'}, dimensions={0} | all-to-all | bytes 16777216 | tf_op jit(solution)/shard_map/all_to_all | solution.py:31
  56.4 0.0 all-gather.3.cloned.1.call-done
  56.4 0.0 copy-start
  56.4 0.0 all-gather.5.cloned.1.call-done
  56.4 7.9 %copy.17 = bf16[4096,1024]{1,0:T(8,128)(2,1)} copy(bf16[4096,1024]{1,0:T(8,128)(2,1)} %bitcast.3) | data formatting | bytes 16777216
  64.3 0.0 copy-done
  64.3 0.0 copy-start.1
  64.3 1.3 %copy.18 = bf16[4096,256]{1,0:T(8,128)(2,1)} copy(bf16[4096,256]{1,0:T(8,128)(2,1)S(1)} %copy-done) | data formatting | bytes 4194304
  65.6 1.0 %copy-done.1 = bf16[4096,256]{1,0:T(8,128)(2,1)S(1)} copy-done((bf16[4096,256]{1,0:T(8,128)(2,1)S(1)}, bf16[4096,256]{1,0:T(8,128)(2,1)}, u32[]{:S(2)}) %copy-start.1) | copy-done | bytes 2097176
  66.6 1.3 %copy.19 = bf16[4096,256]{1,0:T(8,128)(2,1)} copy(bf16[4096,256]{1,0:T(8,128)(2,1)S(1)} %copy-done.1) | data formatting | bytes 4194304
Async XLA Ops:
  7.2 49.2 %all-gather.3.cloned.1.call-start = ((), (), s32[]{:S(2)}) async-start(), calls=%async_computation.1 | async-start | bytes 3145728 | tf_op jit(solution)/shard_map/all_gather | solution.py:34
  7.9 10.4 %copy-start.2 = (f32[2048,256]{1,0:T(8,128)S(1)}, f32[2048,256]{1,0:T(8,128)}, u32[]{:S(2)}) copy-start(f32[2048,256]{1,0:T(8,128)} %param.13) | copy-start | bytes 6291460
  7.9 10.4 %copy-start.3 = (f32[2048,256]{1,0:T(8,128)S(1)}, f32[2048,256]{1,0:T(8,128)}, u32[]{:S(2)}) copy-start(f32[2048,256]{1,0:T(8,128)} %param.12) | copy-start | bytes 6291460
  7.9 10.4 %copy-start.4 = (f32[2048,256]{1,0:T(8,128)S(1)}, f32[2048,256]{1,0:T(8,128)}, u32[]{:S(2)}) copy-start(f32[2048,256]{1,0:T(8,128)} %param.11) | copy-start | bytes 6291460
  7.9 11.1 %copy-start.5 = (f32[2048,256]{1,0:T(8,128)S(1)}, f32[2048,256]{1,0:T(8,128)}, u32[]{:S(2)}) copy-start(f32[2048,256]{1,0:T(8,128)} %param.10) | copy-start | bytes 6291460
  7.9 11.1 %copy-start.6 = (f32[2048]{0:T(1024)S(1)}, f32[2048]{0:T(1024)}, u32[]{:S(2)}) copy-start(f32[2048]{0:T(1024)} %param.14) | copy-start | bytes 24580
  7.9 11.1 %copy-start.7 = (f32[2048]{0:T(1024)S(1)}, f32[2048]{0:T(1024)}, u32[]{:S(2)}) copy-start(f32[2048]{0:T(1024)} %param.15) | copy-start | bytes 24580
  23.6 2.8 %copy-start.9 = (f32[256]{0:T(256)}, f32[256]{0:T(256)S(1)}, u32[]{:S(2)}) copy-start(f32[256]{0:T(256)S(1)} %get-tuple-element.27) | copy-start | bytes 3076
  23.6 2.8 %copy-start.10 = (f32[256]{0:T(256)}, f32[256]{0:T(256)S(1)}, u32[]{:S(2)}) copy-start(f32[256]{0:T(256)S(1)} %get-tuple-element.28) | copy-start | bytes 3076
  23.6 4.0 %copy-start.8 = (f32[1024]{0:T(1024)}, f32[1024]{0:T(1024)S(1)}, u32[]{:S(2)}) copy-start(f32[1024]{0:T(1024)S(1)} %get-tuple-element.26) | copy-start | bytes 12292
  26.4 30.0 %all-gather.5.cloned.1.call-start = ((), (), s32[]{:S(2)}) async-start(), calls=%async_computation.2 | async-start | bytes 3145728 | tf_op jit(solution)/shard_map/all_gather | solution.py:35
  56.4 7.9 %copy-start = (bf16[4096,256]{1,0:T(8,128)(2,1)S(1)}, bf16[4096,256]{1,0:T(8,128)(2,1)}, u32[]{:S(2)}) copy-start(bf16[4096,256]{1,0:T(8,128)(2,1)} %all-gather.3.cloned.1.call-done) | copy-start | bytes 6291460
  64.3 2.3 %copy-start.1 = (bf16[4096,256]{1,0:T(8,128)(2,1)S(1)}, bf16[4096,256]{1,0:T(8,128)(2,1)}, u32[]{:S(2)}) copy-start(bf16[4096,256]{1,0:T(8,128)(2,1)} %all-gather.5.cloned.1.call-done) | copy-start | bytes 6291460
Sparse Core Ops, SparseCore 0:
  26.5 13.1 all-gather.2
  41.8 13.0 all-gather.4
